TPU v7x, 32 devices: a whole 2x2x4 slice. The times are simulated.
32 devices in a mesh: gy: 4 (over y, x), gx: 8 (over z, core).
Axes of the slice: x: 2, y: 2, z: 4, core: 2. Of those that a mesh axis runs over, the one named last changes fastest.
Arguments:
- u_field: float32 [8, 512, 1024], P(None, 'gx', 'gy')
- v_field: float32 [8, 512, 1024], P(None, 'gx', 'gy')
- w_field: float32 [8, 512, 1024], P(None, 'gx', 'gy')
- sep_x: int32 [16], replicated, may hold values from 1 to 128, as said below
- sep_y: int32 [16], replicated, may hold values from 1 to 256, as said below
- sep_z: int32 [16], replicated, may hold values from 1 to 4
Outputs:
- correlation: float32 [3, 16], replicated
Inputs may be any that keep to these rules, and one draw needn't show every extreme that they name: `sep_x`: every separation along x lies in 1 to 128, and 128 is among them in every draw; repeats may occur. `sep_y`: every separation along y lies in 1 to 256, and 256 is among them in every draw; repeats may occur.
All inputs are finite; a program needn't handle non-finite values.
Results may differ from a plain program's by a relative error of at most 0.0003.
Values sent between devices are 32-bit elements; how exact they have to be, the bound alone decides.
A program may use at most 64 MiB of HBM per device.

v0:
```python
import functools

import jax
import jax.numpy as jnp
from jax import lax
from jax.experimental import pallas as pl
from jax.experimental.pallas import tpu as pltpu
from jax.sharding import PartitionSpec as P

MESH = pl.DeviceIdType.MESH
LANES = 128
FIELD_LANES = 32


def split(value):
    high = value.astype(jnp.bfloat16)
    low = (value - high.astype(jnp.float32)).astype(jnp.bfloat16)
    return high, low


def product(left, right, dims):
    dot = functools.partial(
        lax.dot_general, dimension_numbers=(dims, ((), ())), preferred_element_type=jnp.float32
    )
    return dot(left[0], right[0]) + (dot(left[0], right[1]) + dot(left[1], right[0]))


def diagonal_sums(gram, largest):
    rows = gram.shape[0]
    window = largest + LANES
    folded = gram[:LANES, :window]
    for start in range(LANES, rows, LANES):
        folded = folded + gram[start : start + LANES, start : start + window]
    total = folded[:8]
    for start in range(8, LANES, 8):
        total = total + pltpu.roll(folded[start : start + 8], window - start, 1)
    row = lax.broadcasted_iota(jnp.int32, total.shape, 0)
    for bit in (1, 2, 4):
        total = jnp.where((row & bit) != 0, pltpu.roll(total, window - bit, 1), total)
    return total


def kernel(
    n_gx, n_gy,
    u_hbm, v_hbm, w_hbm, sep_x_hbm, sep_y_hbm, sep_z_hbm, out_ref,
    u_own, v_own, w_own, u_wide, v_wide, sep_s, rows,
    plane_sem, load_sem, sep_sem, place_sem, u_send, u_recv, d_send, d_recv, v_send, v_recv,
    row_sem, line_sem, pair_sem,
):
    planes, width_x, width_y = u_own.shape
    seps = sep_s.shape[1]
    quarter, half = planes // 4, planes // 2
    gx, gy = lax.axis_index("gx"), lax.axis_index("gy")
    core, parity = lax.rem(gx, 2), lax.rem(gy, 2)
    chip_first = gx - core

    order = [quarter * part + item for item in range(quarter) for part in range(4)]
    load_u = {
        plane: pltpu.make_async_copy(u_hbm.at[plane], u_own.at[plane], plane_sem.at[plane])
        for plane in order
    }
    load_v = pltpu.make_async_copy(v_hbm, v_own, load_sem.at[0])
    load_w = pltpu.make_async_copy(w_hbm, w_own, load_sem.at[1])
    for plane in order:
        load_u[plane].start()
    load_v.start()

    chip, chips = gx // 2, n_gx // 2
    first, last = chip == 0, chip == chips - 1
    near = gy + 1 - 2 * parity
    far_to = lax.rem(gy + n_gy - 2 + 4 * parity, n_gy)
    far_from = lax.rem(gy + n_gy + 2 - 4 * parity, n_gy)
    barrier = pltpu.get_barrier_semaphore()

    def greet(semaphore, **device):
        pl.semaphore_signal(semaphore, inc=1, device_id=device, device_id_type=MESH)

    @pl.when(~first)
    def _():
        greet(barrier, gx=chip_first - 2)
        greet(barrier, gx=chip_first - 1)

    @pl.when(~last)
    def _():
        greet(barrier, gx=chip_first + 2)
        greet(barrier, gx=chip_first + 3)

    greet(barrier, gx=chip_first + 1 - core)
    greet(barrier, gy=near)
    greet(barrier, gy=far_from)
    load_w.start()
    sep_loads = [
        pltpu.make_async_copy(ref, sep_s.at[index], sep_sem.at[index])
        for index, ref in enumerate((sep_x_hbm, sep_y_hbm, sep_z_hbm))
    ]
    places = []
    for side in range(2):
        places.append(pltpu.make_async_copy(
            u_hbm.at[pl.ds(half * side + quarter * core, quarter)],
            u_wide.at[side, :, 2 * side + core],
            place_sem.at[side],
        ))
    places.append(pltpu.make_async_copy(
        v_hbm.at[pl.ds(half * parity, half)], v_wide.at[2 * parity], place_sem.at[2]
    ))
    for copy in places + sep_loads:
        copy.start()

    u_copies = {}
    for item in range(quarter):
        for other in range(2):
            for side in range(2):
                target = lax.rem(chip_first + (n_gx - 2 if side == 0 else 2), n_gx)
                u_copies[side, item, other] = (pltpu.make_async_remote_copy(
                    src_ref=u_own.at[half * side + quarter * other + item],
                    dst_ref=u_wide.at[side, item, (2 if side == 0 else 0) + core],
                    send_sem=u_send.at[side, item, other],
                    recv_sem=u_recv.at[side, item, core],
                    device_id={"gx": target + other},
                    device_id_type=MESH,
                ))
    d_copies = []
    for side in range(2):
        d_copies.append(pltpu.make_async_remote_copy(
            src_ref=u_own.at[pl.ds(half * side + quarter * (1 - core), quarter)],
            dst_ref=u_wide.at[side, :, 2 * side + core],
            send_sem=d_send.at[side],
            recv_sem=d_recv.at[side],
            device_id={"gx": chip_first + 1 - core},
            device_id_type=MESH,
        ))
    v_copies = []
    for item in range(half):
        v_copies.append(pltpu.make_async_remote_copy(
            src_ref=v_own.at[half * (1 - parity) + item],
            dst_ref=v_wide.at[1, item],
            send_sem=v_send.at[0, item],
            recv_sem=v_recv.at[0, item],
            device_id={"gy": near},
            device_id_type=MESH,
        ))
        v_copies.append(pltpu.make_async_remote_copy(
            src_ref=v_own.at[half * parity + item],
            dst_ref=v_wide.at[2 - 2 * parity, item],
            send_sem=v_send.at[1, item],
            recv_sem=v_recv.at[1, item],
            device_id={"gy": far_to},
            device_id_type=MESH,
        ))

    for plane in order[:4]:
        load_u[plane].wait()
    inner = jnp.where(first, 0, 2) + jnp.where(last, 0, 2)
    pl.semaphore_wait(barrier, inner + 3)

    def start_u(side, items, at_end):
        wraps = first if side == 0 else last

        @pl.when(wraps if at_end else ~wraps)
        def _():
            for item in items:
                for other in range(2):
                    u_copies[side, item, other].start()

    ends = first | last
    for side in range(2):
        start_u(side, range(1), False)
    for plane in order[4:]:
        load_u[plane].wait()
    @pl.when(~ends)
    def _():
        for side in range(2):
            for item in range(1, quarter):
                for other in range(2):
                    u_copies[side, item, other].start()
    load_v.wait()
    for copy in v_copies + d_copies:
        copy.start()

    up, down = line_sem.at[0], line_sem.at[1]

    @pl.when(chip == 1)
    def _():
        greet(up, gx=gx + 2)

    @pl.when(chip == chips - 2)
    def _():
        greet(down, gx=gx - 2)

    @pl.when(chip >= 2)
    def _():
        pl.semaphore_wait(up, 1)

    @pl.when((chip >= 2) & (chip <= chips - 2))
    def _():
        greet(up, gx=gx + 2)

    @pl.when(chip <= chips - 3)
    def _():
        pl.semaphore_wait(down, 1)

    @pl.when((chip >= 1) & (chip <= chips - 3))
    def _():
        greet(down, gx=gx - 2)

    for side in range(2):
        start_u(side, range(quarter), True)
    @pl.when(ends)
    def _():
        for side in range(2):
            start_u(side, range(1, quarter), False)

    greet(pair_sem.at[0], gy=near)
    pl.semaphore_wait(pair_sem.at[0], 1)
    for hop in range(1, n_gy // 2):
        greet(pair_sem.at[hop], gy=far_from)
        pl.semaphore_wait(pair_sem.at[hop], 1)

    for copy in sep_loads:
        copy.wait()
    lane = lax.broadcasted_iota(jnp.int32, (1, LANES), 1)
    lag_row = jnp.full((1, LANES), -1, jnp.int32)
    for field in range(3):
        for index in range(seps):
            lag_row = jnp.where(lane == FIELD_LANES * field + index, sep_s[field, index], lag_row)
        lag_row = jnp.where(lane == FIELD_LANES * field + seps, 0, lag_row)

    def picker(field, lags):
        of_field = (lane >= FIELD_LANES * field) & (lane < FIELD_LANES * (field + 1))
        wanted = jnp.where(of_field, lag_row, -1)
        lag = lax.broadcasted_iota(jnp.int32, (lags, LANES), 0)
        return jnp.where(lag == wanted, 1.0, 0.0).astype(jnp.bfloat16)

    pick_x = picker(0, 2 * width_x + LANES)
    pick_y = picker(1, width_y + LANES)

    def pick(sums, chosen):
        high = sums.astype(jnp.bfloat16).astype(jnp.float32)
        middle = (sums - high).astype(jnp.bfloat16).astype(jnp.float32)
        low = (sums - high) - middle
        parts = jnp.concatenate([high, middle, low], axis=0).astype(jnp.bfloat16)
        return jnp.dot(parts, chosen, preferred_element_type=jnp.float32)

    load_w.wait()
    lags_z = half + 1
    tile_rows = 8

    def z_step(index, carry):
        start = pl.multiple_of(index * tile_rows, tile_rows)
        rows = [w_own[plane, pl.ds(start, tile_rows), :] for plane in range(planes)]
        return tuple(
            carry[lag] + sum(rows[plane] * rows[plane + lag] for plane in range(planes - lag))
            for lag in range(lags_z)
        )

    zero = jnp.zeros((tile_rows, width_y), jnp.float32)
    z_sums = lax.fori_loop(0, width_x // tile_rows, z_step, (zero,) * lags_z)
    row_z = jnp.zeros((1, LANES), jnp.float32)
    for lag in range(lags_z):
        row_z = jnp.where(lag_row == lag, jnp.sum(z_sums[lag]), row_z)
    row_z = jnp.where((lane >= 2 * FIELD_LANES) & (lane < 3 * FIELD_LANES), row_z, 0.0)

    for copy in places:
        copy.wait()
    for copy in v_copies:
        copy.wait_recv()
    cells = half * width_x
    wide = v_wide[...].reshape(3 * cells, width_y)
    high, low = split(wide)
    left = (high[: 2 * cells], low[: 2 * cells])
    gram_0 = product(left, left, ((0,), (0,)))
    gram_1 = product(left, (high[cells:], low[cells:]), ((0,), (0,)))
    gram_y = jnp.concatenate([gram_0, gram_1], axis=1)
    rest = jnp.sum(pick(diagonal_sums(gram_y, width_y), pick_y), axis=0, keepdims=True) + row_z

    for copy in d_copies:
        copy.wait_recv()
    gram_x = None
    for item in range(quarter):
        for side in range(2):
            for sender in range(2):
                slot = (2 if side == 0 else 0) + sender
                pltpu.make_async_remote_copy(
                    src_ref=u_own.at[0],
                    dst_ref=u_wide.at[side, item, slot],
                    send_sem=u_send.at[side, item, sender],
                    recv_sem=u_recv.at[side, item, sender],
                    device_id={"gx": chip_first + 1 - core},
                    device_id_type=MESH,
                ).wait_recv()
            pair = split(u_wide[side, item].reshape(4 * width_x, width_y))
            lower = (pair[0][: 2 * width_x], pair[1][: 2 * width_x])
            term = product(lower, pair, ((1,), (1,)))
            gram_x = term if gram_x is None else gram_x + term
    mine = jnp.sum(pick(diagonal_sums(gram_x, 2 * width_x), pick_x), axis=0, keepdims=True) + rest

    count = n_gx * n_gy
    me = gx * n_gy + gy
    rows[me] = mine

    flips = [(1 - 2 * lax.rem(me // (1 << bit), 2)) * (1 << bit) for bit in range(count.bit_length() - 1)]
    by_flips = count == 1 << len(flips)

    def to_device(step):
        if by_flips and isinstance(step, int):
            peer = me + sum(flip for bit, flip in enumerate(flips) if step >> bit & 1)
        else:
            peer = lax.rem(me + step, count)
        return pltpu.make_async_remote_copy(
            src_ref=rows.at[me],
            dst_ref=rows.at[me],
            send_sem=row_sem.at[0],
            recv_sem=row_sem.at[1],
            device_id={"gx": peer // n_gy, "gy": lax.rem(peer, n_gy)},
            device_id_type=MESH,
        )

    if count <= 64:
        for step in reversed(range(1, count)):
            to_device(step).start()
    else:
        lax.fori_loop(1, count, lambda step, _: to_device(step).start(), None)
    all_rows = pltpu.make_async_remote_copy(
        src_ref=rows.at[pl.ds(0, count - 1)],
        dst_ref=rows.at[pl.ds(0, count - 1)],
        send_sem=row_sem.at[0],
        recv_sem=row_sem.at[1],
        device_id={"gx": chip_first + 1 - core},
        device_id_type=MESH,
    )
    all_rows.wait_recv()
    total = jnp.sum(rows[...], axis=0)

    for field in range(3):
        base = FIELD_LANES * field
        row = total[:, base : base + seps] / total[:, base + seps : base + seps + 1]
        if field == 2:
            lag = lag_row[:, base : base + seps].astype(jnp.float32)
            row = row * (jnp.float32(planes) / (jnp.float32(planes) - lag))
        out_ref[field : field + 1, :] = row

    all_rows.wait_send()
    for copy in list(u_copies.values()) + v_copies + d_copies:
        copy.wait_send()


def local(n_gx, n_gy, u_field, v_field, w_field, sep_x, sep_y, sep_z):
    planes, width_x, width_y = u_field.shape
    quarter, half = planes // 4, planes // 2
    seps = sep_x.shape[0]
    dma = pltpu.SemaphoreType.DMA
    block = (planes, width_x, width_y)
    return pl.pallas_call(
        functools.partial(kernel, n_gx, n_gy),
        out_shape=pltpu.VMEM((3, seps), jnp.float32),
        in_specs=[pl.BlockSpec(memory_space=pl.ANY)] * 6,
        out_specs=pl.BlockSpec(memory_space=pltpu.VMEM),
        scratch_shapes=[
            pltpu.VMEM(block, jnp.float32),
            pltpu.VMEM(block, jnp.float32),
            pltpu.VMEM(block, jnp.float32),
            pltpu.VMEM((2, quarter, 4, width_x, width_y), jnp.float32),
            pltpu.VMEM((3, half, width_x, width_y), jnp.float32),
            pltpu.SMEM((3, seps), jnp.int32),
            pltpu.VMEM((n_gx * n_gy, 1, LANES), jnp.float32),
            dma((planes,)),
            dma((2,)),
            dma((3,)),
            dma((3,)),
            dma((2, quarter, 2)),
            dma((2, quarter, 2)),
            dma((2,)),
            dma((2,)),
            dma((2, half)),
            dma((2, half)),
            dma((2,)),
            pltpu.SemaphoreType.REGULAR((2,)),
            pltpu.SemaphoreType.REGULAR((n_gy // 2,)),
        ],
        compiler_params=pltpu.CompilerParams(collective_id=0, has_side_effects=True),
    )(u_field, v_field, w_field, sep_x, sep_y, sep_z)


def solution(mesh):
    return jax.shard_map(
        functools.partial(local, mesh.shape["gx"], mesh.shape["gy"]),
        mesh=mesh,
        in_specs=(P(None, "gx", "gy"), P(None, "gx", "gy"), P(None, "gx", "gy"), P(), P(), P()),
        out_specs=P(),
        check_vma=False,
    )
```

profile of v0, /device:TPU:0, one launch (start us, length us, event | category | flops | bytes accessed | tf_op | source)
XLA Modules:
  0.0 24.0 jit_solution(6707488626054753639)
XLA Ops:
  0.0 23.4 %shard_map.64 = f32[3,16]{1,0:T(4,128)S(1)} custom-call(f32[8,64,256]{2,1,0:T(8,128)} %u_hbm.1, f32[8,64,256]{2,1,0:T(8,128)} %v_hbm.1, f32[8,64,256]{2,1,0:T(8,128)} %w_hbm.1, s32[16]{0:T(128)} %sep_x_hbm.1, s32[16]{0:T(128)} %sep_y_hbm.1, s32[16]{0:T(128)} %sep_z_hbm.1), custom_call_target="tpu_custom_call" | custom-call | tf_op jit(solution)/shard_map/pallas_call | solution.py:353
  23.4 0.6 %copy.8 = f32[3,16]{1,0:T(4,128)} copy(f32[3,16]{1,0:T(4,128)S(1)} %shard_map.64) | data formatting | bytes 384
where the time goes:
time: 24.2 us; the launch traced here: 24 us
  Pallas kernels  23.4 us (97%)
  local copies, waits for them, and re-layouts  0.58 us (2%)
    pallas_call x1, Pallas kernels, local(): pl.pallas_call(functools.partial(kernel, n_gx, n_gy), out_shape=pltpu.VME...  23.4 us
    unnamed x1, local copies, waits for them, and re-layouts  0.58 us

commit v1 on v0

v1 whole, which is shorter than its diff:
```python
import functools

import jax
import jax.numpy as jnp
from jax import lax
from jax.experimental import pallas as pl
from jax.experimental.pallas import tpu as pltpu
from jax.sharding import PartitionSpec as P

MESH = pl.DeviceIdType.MESH
LANES = 128
FIELD_LANES = 32


def split(value):
    high = value.astype(jnp.bfloat16)
    low = (value - high.astype(jnp.float32)).astype(jnp.bfloat16)
    return high, low


def product(left, right, dims):
    dot = functools.partial(
        lax.dot_general, dimension_numbers=(dims, ((), ())), preferred_element_type=jnp.float32
    )
    return dot(left[0], right[0]) + (dot(left[0], right[1]) + dot(left[1], right[0]))


def lag_sums(gram, lags, largest):
    rows = gram.shape[0]
    window = largest + LANES
    folded = gram[:LANES, :window]
    for start in range(LANES, rows, LANES):
        folded = folded + gram[start : start + LANES, start : start + window]
    at = jnp.broadcast_to(lags, (8, LANES)) + lax.broadcasted_iota(jnp.int32, (8, LANES), 0)
    total = None
    for start in range(0, LANES, 8):
        index = at + start
        lane, tile = index & (LANES - 1), index // LANES
        part = None
        for column in range(0, window, LANES):
            piece = jnp.take_along_axis(folded[start : start + 8, column : column + LANES], lane, axis=1)
            part = piece if part is None else jnp.where(tile == column // LANES, piece, part)
        total = part if total is None else total + part
    return jnp.where(lags < 0, 0.0, jnp.sum(total, axis=0, keepdims=True))


def kernel(
    n_gx, n_gy,
    u_hbm, v_hbm, w_hbm, sep_x_hbm, sep_y_hbm, sep_z_hbm, out_ref,
    u_own, v_own, w_own, u_wide, v_wide, sep_s, rows,
    plane_sem, load_sem, sep_sem, send_sem, u_recv, recv_sem, row_sem, line_sem, pair_sem,
):
    planes, width_x, width_y = v_own.shape
    seps = sep_s.shape[1]
    quarter, half = planes // 4, planes // 2
    gx, gy = lax.axis_index("gx"), lax.axis_index("gy")
    core, parity = lax.rem(gx, 2), lax.rem(gy, 2)
    chip_first = gx - core

    load_u = [
        pltpu.make_async_copy(u_hbm.at[item], u_own.at[item], plane_sem.at[item])
        for item in range(quarter)
    ]
    load_v = pltpu.make_async_copy(v_hbm, v_own, load_sem.at[0])
    load_w = pltpu.make_async_copy(w_hbm, w_own, load_sem.at[1])
    for copy in load_u:
        copy.start()
    load_v.start()

    chip, chips = gx // 2, n_gx // 2
    first, last = chip == 0, chip == chips - 1
    near = gy + 1 - 2 * parity
    far_to = lax.rem(gy + n_gy - 2 + 4 * parity, n_gy)
    far_from = lax.rem(gy + n_gy + 2 - 4 * parity, n_gy)
    barrier = pltpu.get_barrier_semaphore()

    def greet(semaphore, **device):
        pl.semaphore_signal(semaphore, inc=1, device_id=device, device_id_type=MESH)

    @pl.when(~first)
    def _():
        greet(barrier, gx=chip_first - 2)
        greet(barrier, gx=chip_first - 1)

    @pl.when(~last)
    def _():
        greet(barrier, gx=chip_first + 2)
        greet(barrier, gx=chip_first + 3)

    greet(barrier, gx=chip_first + 1 - core)
    greet(barrier, gy=near)
    greet(barrier, gy=far_from)
    load_w.start()
    sep_loads = [
        pltpu.make_async_copy(ref, sep_s.at[index], sep_sem.at[0])
        for index, ref in enumerate((sep_x_hbm, sep_y_hbm, sep_z_hbm))
    ]
    places = []
    for side in range(2):
        places.append(pltpu.make_async_copy(
            u_hbm.at[:, side, core],
            u_wide.at[side, :, 2 * side + core],
            load_sem.at[2],
        ))
    places.append(pltpu.make_async_copy(
        v_hbm.at[pl.ds(half * parity, half)], v_wide.at[2 * parity], load_sem.at[2]
    ))
    for copy in places + sep_loads:
        copy.start()

    u_copies = {}
    for item in range(quarter):
        for other in range(2):
            for side in range(2):
                target = lax.rem(chip_first + (n_gx - 2 if side == 0 else 2), n_gx)
                u_copies[side, item, other] = (pltpu.make_async_remote_copy(
                    src_ref=u_own.at[item, side, other],
                    dst_ref=u_wide.at[side, item, (2 if side == 0 else 0) + core],
                    send_sem=send_sem.at[0],
                    recv_sem=u_recv.at[side, item],
                    device_id={"gx": target + other},
                    device_id_type=MESH,
                ))
    d_copies = []
    for side in range(2):
        d_copies.append(pltpu.make_async_remote_copy(
            src_ref=u_own.at[:, side, 1 - core],
            dst_ref=u_wide.at[side, :, 2 * side + core],
            send_sem=send_sem.at[2],
            recv_sem=recv_sem.at[0],
            device_id={"gx": chip_first + 1 - core},
            device_id_type=MESH,
        ))
    v_copies = []
    for item in range(half):
        v_copies.append(pltpu.make_async_remote_copy(
            src_ref=v_own.at[half * (1 - parity) + item],
            dst_ref=v_wide.at[1, item],
            send_sem=send_sem.at[1],
            recv_sem=recv_sem.at[1],
            device_id={"gy": near},
            device_id_type=MESH,
        ))
        v_copies.append(pltpu.make_async_remote_copy(
            src_ref=v_own.at[half * parity + item],
            dst_ref=v_wide.at[2 - 2 * parity, item],
            send_sem=send_sem.at[1],
            recv_sem=recv_sem.at[1],
            device_id={"gy": far_to},
            device_id_type=MESH,
        ))

    load_u[0].wait()
    inner = jnp.where(first, 0, 2) + jnp.where(last, 0, 2)
    pl.semaphore_wait(barrier, inner + 3)

    def start_u(side, items, at_end):
        wraps = first if side == 0 else last

        @pl.when(wraps if at_end else ~wraps)
        def _():
            for item in items:
                for other in range(2):
                    u_copies[side, item, other].start()

    ends = first | last
    for side in range(2):
        start_u(side, range(1), False)
    for copy in load_u[1:]:
        copy.wait()
    @pl.when(~ends)
    def _():
        for side in range(2):
            for item in range(1, quarter):
                for other in range(2):
                    u_copies[side, item, other].start()
    load_v.wait()
    for copy in v_copies + d_copies:
        copy.start()

    up, down = line_sem.at[0], line_sem.at[1]

    @pl.when(chip == 1)
    def _():
        greet(up, gx=gx + 2)

    @pl.when(chip == chips - 2)
    def _():
        greet(down, gx=gx - 2)

    @pl.when(chip >= 2)
    def _():
        pl.semaphore_wait(up, 1)

    @pl.when((chip >= 2) & (chip <= chips - 2))
    def _():
        greet(up, gx=gx + 2)

    @pl.when(chip <= chips - 3)
    def _():
        pl.semaphore_wait(down, 1)

    @pl.when((chip >= 1) & (chip <= chips - 3))
    def _():
        greet(down, gx=gx - 2)

    for side in range(2):
        start_u(side, range(quarter), True)
    @pl.when(ends)
    def _():
        for side in range(2):
            start_u(side, range(1, quarter), False)

    greet(pair_sem.at[0], gy=near)
    pl.semaphore_wait(pair_sem.at[0], 1)
    for hop in range(1, n_gy // 2):
        greet(pair_sem.at[hop], gy=far_from)
        pl.semaphore_wait(pair_sem.at[hop], 1)

    pltpu.make_async_copy(sep_s, sep_s, sep_sem.at[0]).wait()
    lane = lax.broadcasted_iota(jnp.int32, (1, LANES), 1)
    lag_row = jnp.full((1, LANES), -1, jnp.int32)
    for field in range(3):
        for index in range(seps):
            lag_row = jnp.where(lane == FIELD_LANES * field + index, sep_s[field, index], lag_row)
        lag_row = jnp.where(lane == FIELD_LANES * field + seps, 0, lag_row)

    def lags_of(field):
        of_field = (lane >= FIELD_LANES * field) & (lane < FIELD_LANES * (field + 1))
        return jnp.where(of_field, lag_row, -1)

    lags_x, lags_y = lags_of(0), lags_of(1)

    load_w.wait()
    lags_z = half + 1
    tile_rows = 8

    def z_step(index, carry):
        start = pl.multiple_of(index * tile_rows, tile_rows)
        rows = [w_own[plane, pl.ds(start, tile_rows), :] for plane in range(planes)]
        return tuple(
            carry[lag] + sum(rows[plane] * rows[plane + lag] for plane in range(planes - lag))
            for lag in range(lags_z)
        )

    zero = jnp.zeros((tile_rows, width_y), jnp.float32)
    z_sums = lax.fori_loop(0, width_x // tile_rows, z_step, (zero,) * lags_z)
    row_z = jnp.zeros((1, LANES), jnp.float32)
    for lag in range(lags_z):
        row_z = jnp.where(lag_row == lag, jnp.sum(z_sums[lag]), row_z)
    row_z = jnp.where((lane >= 2 * FIELD_LANES) & (lane < 3 * FIELD_LANES), row_z, 0.0)

    pltpu.make_async_copy(v_hbm, v_own, load_sem.at[2]).wait()

    def arrived(ref, send, recv):
        return pltpu.make_async_remote_copy(
            src_ref=ref,
            dst_ref=ref,
            send_sem=send,
            recv_sem=recv,
            device_id={"gx": chip_first + 1 - core},
            device_id_type=MESH,
        )

    all_u = arrived(u_own, send_sem.at[0], recv_sem.at[0])
    all_v = arrived(v_own, send_sem.at[1], recv_sem.at[1])
    all_d = arrived(u_wide.at[0, :, pl.ds(0, 2)], send_sem.at[2], recv_sem.at[0])
    all_v.wait_recv()
    cells = half * width_x
    wide = v_wide[...].reshape(3 * cells, width_y)
    high, low = split(wide)
    left = (high[: 2 * cells], low[: 2 * cells])
    gram_0 = product(left, left, ((0,), (0,)))
    gram_1 = product(left, (high[cells:], low[cells:]), ((0,), (0,)))
    gram_y = jnp.concatenate([gram_0, gram_1], axis=1)
    rest = lag_sums(gram_y, lags_y, width_y) + row_z

    all_d.wait_recv()
    gram_x = None
    for item in range(quarter):
        for side in range(2):
            theirs = u_wide.at[side, item, pl.ds(2 - 2 * side, 2)]
            arrived(theirs, send_sem.at[0], u_recv.at[side, item]).wait_recv()
            pair = split(u_wide[side, item].reshape(4 * width_x, width_y))
            lower = (pair[0][: 2 * width_x], pair[1][: 2 * width_x])
            term = product(lower, pair, ((1,), (1,)))
            gram_x = term if gram_x is None else gram_x + term
    mine = lag_sums(gram_x, lags_x, 2 * width_x) + rest

    count = n_gx * n_gy
    me = gx * n_gy + gy
    rows[me] = mine

    place = gy * n_gx + gx

    def to_device(step):
        peer = jnp.where(step < place, step, step + 1)
        return pltpu.make_async_remote_copy(
            src_ref=rows.at[me],
            dst_ref=rows.at[me],
            send_sem=row_sem.at[0],
            recv_sem=row_sem.at[1],
            device_id={"gx": lax.rem(peer, n_gx), "gy": peer // n_gx},
            device_id_type=MESH,
        )

    if count <= 64:
        for step in range(count - 1):
            to_device(step).start()
    else:
        lax.fori_loop(0, count - 1, lambda step, _: to_device(step).start(), None)
    all_rows = arrived(rows.at[pl.ds(0, count - 1)], row_sem.at[0], row_sem.at[1])
    for copy in (all_u, all_v, all_d):
        copy.wait_send()
    all_rows.wait_recv()
    total = jnp.sum(rows[...], axis=0)

    for field in range(3):
        base = FIELD_LANES * field
        row = total[:, base : base + seps] / total[:, base + seps : base + seps + 1]
        if field == 2:
            lag = lag_row[:, base : base + seps].astype(jnp.float32)
            row = row * (jnp.float32(planes) / (jnp.float32(planes) - lag))
        out_ref[field : field + 1, :] = row

    all_rows.wait_send()


def local(n_gx, n_gy, u_field, v_field, w_field, sep_x, sep_y, sep_z):
    planes, width_x, width_y = u_field.shape
    quarter, half = planes // 4, planes // 2
    seps = sep_x.shape[0]
    dma = pltpu.SemaphoreType.DMA
    block = (planes, width_x, width_y)
    return pl.pallas_call(
        functools.partial(kernel, n_gx, n_gy),
        out_shape=pltpu.VMEM((3, seps), jnp.float32),
        in_specs=[pl.BlockSpec(memory_space=pl.ANY)] * 6,
        out_specs=pl.BlockSpec(memory_space=pltpu.VMEM),
        scratch_shapes=[
            pltpu.VMEM((quarter, 2, 2, width_x, width_y), jnp.float32),
            pltpu.VMEM(block, jnp.float32),
            pltpu.VMEM(block, jnp.float32),
            pltpu.VMEM((2, quarter, 4, width_x, width_y), jnp.float32),
            pltpu.VMEM((3, half, width_x, width_y), jnp.float32),
            pltpu.SMEM((3, seps), jnp.int32),
            pltpu.VMEM((n_gx * n_gy, 1, LANES), jnp.float32),
            dma((quarter,)),
            dma((3,)),
            dma((1,)),
            dma((3,)),
            dma((2, quarter)),
            dma((2,)),
            dma((2,)),
            pltpu.SemaphoreType.REGULAR((2,)),
            pltpu.SemaphoreType.REGULAR((n_gy // 2,)),
        ],
        compiler_params=pltpu.CompilerParams(collective_id=0, has_side_effects=True),
    )(u_field.reshape(quarter, 2, 2, width_x, width_y), v_field, w_field, sep_x, sep_y, sep_z)


def solution(mesh):
    return jax.shard_map(
        functools.partial(local, mesh.shape["gx"], mesh.shape["gy"]),
        mesh=mesh,
        in_specs=(P(None, "gx", "gy"), P(None, "gx", "gy"), P(None, "gx", "gy"), P(), P(), P()),
        out_specs=P(),
        check_vma=False,
    )
```

time: 24.2 us -> 23.5 us (0.971)
  Pallas kernels: 23.4 us -> 22.7 us
    pallas_call x1, Pallas kernels: 23.4 us -> 22.7 us  [local(): pl.pallas_call(functools.partial(kernel, n_gx, n_gy), out_shape=pltpu.VME...]
where the time goes in v1:
time: 23.5 us; the launch traced here: 23.3 us
  Pallas kernels  22.7 us (97%)
  local copies, waits for them, and re-layouts  0.58 us (2%)
    pallas_call x1, Pallas kernels, local(): pl.pallas_call(functools.partial(kernel, n_gx, n_gy), out_shape=pltpu.VME...  22.7 us
    unnamed x1, local copies, waits for them, and re-layouts  0.58 us

profile of v1, /device:TPU:0, one launch (start us, length us, event | category | flops | bytes accessed | tf_op | source)
XLA Modules:
  0.0 23.3 jit_solution(9568831392543585594)
XLA Ops:
  0.0 22.7 %shard_map.64 = f32[3,16]{1,0:T(4,128)S(1)} custom-call(f32[2,2,2,64,256]{4,3,2,1,0:T(8,128)} %bitcast.1, f32[8,64,256]{2,1,0:T(8,128)} %v_hbm.1, f32[8,64,256]{2,1,0:T(8,128)} %w_hbm.1, s32[16]{0:T(128)} %sep_x_hbm.1, s32[16]{0:T(128)} %sep_y_hbm.1, s32[16]{0:T(128)} %sep_z_hbm.1), custom_call_target="tpu_custom_call" | custom-call | tf_op jit(solution)/shard_map/pallas_call | solution.py:335
  22.7 0.6 %copy.8 = f32[3,16]{1,0:T(4,128)} copy(f32[3,16]{1,0:T(4,128)S(1)} %shard_map.64) | data formatting | bytes 384

commit v2 on v1

--- a/solution.py
+++ b/solution.py
@@ -10,6 +10,7 @@
 MESH = pl.DeviceIdType.MESH
 LANES = 128
 FIELD_LANES = 32
+GUEST_CORE = 0
 
 
 def split(value):
@@ -25,34 +26,38 @@
     return dot(left[0], right[0]) + (dot(left[0], right[1]) + dot(left[1], right[0]))
 
 
-def lag_sums(gram, lags, largest):
-    rows = gram.shape[0]
-    window = largest + LANES
-    folded = gram[:LANES, :window]
-    for start in range(LANES, rows, LANES):
-        folded = folded + gram[start : start + LANES, start : start + window]
-    at = jnp.broadcast_to(lags, (8, LANES)) + lax.broadcasted_iota(jnp.int32, (8, LANES), 0)
+def lag_sums(gram, offset):
+    rows, columns = gram.shape
+    at = jnp.broadcast_to(offset, (8, LANES)) + lax.broadcasted_iota(jnp.int32, (8, LANES), 0)
     total = None
-    for start in range(0, LANES, 8):
+    for start in range(0, rows, 8):
         index = at + start
-        lane, tile = index & (LANES - 1), index // LANES
-        part = None
-        for column in range(0, window, LANES):
-            piece = jnp.take_along_axis(folded[start : start + 8, column : column + LANES], lane, axis=1)
-            part = piece if part is None else jnp.where(tile == column // LANES, piece, part)
+        lane = index & (LANES - 1)
+        part = jnp.zeros((8, LANES), jnp.float32)
+        for column in range(0, columns, LANES):
+            piece = jnp.take_along_axis(gram[start : start + 8, column : column + LANES], lane, axis=1)
+            part = jnp.where((index >= column) & (index < column + LANES), piece, part)
         total = part if total is None else total + part
-    return jnp.where(lags < 0, 0.0, jnp.sum(total, axis=0, keepdims=True))
+    return total
+
+
+def folded(gram, window):
+    total = gram[:LANES, :window]
+    for start in range(LANES, gram.shape[0], LANES):
+        total = total + gram[start : start + LANES, start : start + window]
+    return total
 
 
 def kernel(
     n_gx, n_gy,
     u_hbm, v_hbm, w_hbm, sep_x_hbm, sep_y_hbm, sep_z_hbm, out_ref,
-    u_own, v_own, w_own, u_wide, v_wide, sep_s, rows,
+    u_own, v_own, w_own, u_wide, u_guest, guest_sums, v_wide, sep_s, rows,
     plane_sem, load_sem, sep_sem, send_sem, u_recv, recv_sem, row_sem, line_sem, pair_sem,
 ):
     planes, width_x, width_y = v_own.shape
     seps = sep_s.shape[1]
     quarter, half = planes // 4, planes // 2
+    SHARED = (1, quarter - 1, 1)
     gx, gy = lax.axis_index("gx"), lax.axis_index("gy")
     core, parity = lax.rem(gx, 2), lax.rem(gy, 2)
     chip_first = gx - core
@@ -86,6 +91,13 @@
     def _():
         greet(barrier, gx=chip_first + 2)
         greet(barrier, gx=chip_first + 3)
+
+    gives, takes = gy == n_gy - 1, (gy == 0) & (core == GUEST_CORE)
+
+    @pl.when(takes)
+    def _():
+        greet(barrier, gx=chip_first, gy=n_gy - 1)
+        greet(barrier, gx=chip_first + 1, gy=n_gy - 1)
 
     greet(barrier, gx=chip_first + 1 - core)
     greet(barrier, gy=near)
@@ -108,19 +120,62 @@
     for copy in places + sep_loads:
         copy.start()
 
-    u_copies = {}
-    for item in range(quarter):
-        for other in range(2):
-            for side in range(2):
-                target = lax.rem(chip_first + (n_gx - 2 if side == 0 else 2), n_gx)
-                u_copies[side, item, other] = (pltpu.make_async_remote_copy(
-                    src_ref=u_own.at[item, side, other],
-                    dst_ref=u_wide.at[side, item, (2 if side == 0 else 0) + core],
-                    send_sem=send_sem.at[0],
-                    recv_sem=u_recv.at[side, item],
-                    device_id={"gx": target + other},
-                    device_id_type=MESH,
-                ))
+    short = gives & (core == 1)
+    part = pl.ds(width_y // 2, width_y // 2)
+    kept = pl.ds(0, width_y // 2)
+
+    guest_sums[...] = jnp.zeros_like(guest_sums)
+
+    def u_copy(side, item, other, lanes):
+        target = lax.rem(chip_first + (n_gx - 2 if side == 0 else 2), n_gx)
+        return pltpu.make_async_remote_copy(
+            src_ref=u_own.at[item, side, other, :, lanes],
+            dst_ref=u_wide.at[side, item, (2 if side == 0 else 0) + core, :, lanes],
+            send_sem=send_sem.at[3 if (side, item, other) == SHARED else 0],
+            recv_sem=u_recv.at[side, item],
+            device_id={"gx": target + other},
+            device_id_type=MESH,
+        )
+
+    def start_copy(side, item, other):
+        if (side, item, other) != SHARED:
+            u_copy(side, item, other, pl.ds(0, width_y)).start()
+            return
+
+        @pl.when(gives)
+        def _():
+            u_copy(side, item, other, kept).start()
+
+        @pl.when(~(gives | takes))
+        def _():
+            u_copy(side, item, other, pl.ds(0, width_y)).start()
+
+    def arrived(ref, send, recv):
+        return pltpu.make_async_remote_copy(
+            src_ref=ref,
+            dst_ref=ref,
+            send_sem=send,
+            recv_sem=recv,
+            device_id={"gx": chip_first + 1 - core},
+            device_id_type=MESH,
+        )
+
+    give = pltpu.make_async_remote_copy(
+        src_ref=u_own.at[quarter - 1, 1, 1, :, part],
+        dst_ref=u_guest.at[core],
+        send_sem=send_sem.at[3],
+        recv_sem=recv_sem.at[2],
+        device_id={"gx": chip_first + GUEST_CORE, "gy": 0},
+        device_id_type=MESH,
+    )
+    guest_on = pltpu.make_async_remote_copy(
+        src_ref=u_guest.at[pl.ds(0, 2)],
+        dst_ref=u_guest.at[pl.ds(2, 2)],
+        send_sem=send_sem.at[4],
+        recv_sem=recv_sem.at[3],
+        device_id={"gx": lax.rem(chip_first + 2, n_gx) + GUEST_CORE},
+        device_id_type=MESH,
+    )
     d_copies = []
     for side in range(2):
         d_copies.append(pltpu.make_async_remote_copy(
@@ -150,30 +205,31 @@
             device_id_type=MESH,
         ))
 
-    load_u[0].wait()
+    for copy in load_u:
+        copy.wait()
     inner = jnp.where(first, 0, 2) + jnp.where(last, 0, 2)
-    pl.semaphore_wait(barrier, inner + 3)
-
-    def start_u(side, items, at_end):
+    pl.semaphore_wait(barrier, inner + jnp.where(gives, 4, 3))
+
+    def start_u(side, other, at_end):
         wraps = first if side == 0 else last
 
         @pl.when(wraps if at_end else ~wraps)
         def _():
-            for item in items:
-                for other in range(2):
-                    u_copies[side, item, other].start()
+            for item in range(quarter):
+                start_copy(side, item, other)
 
     ends = first | last
     for side in range(2):
-        start_u(side, range(1), False)
-    for copy in load_u[1:]:
-        copy.wait()
+        start_u(side, 0, False)
     @pl.when(~ends)
     def _():
-        for side in range(2):
-            for item in range(1, quarter):
-                for other in range(2):
-                    u_copies[side, item, other].start()
+        for item in range(quarter):
+            for side in range(2):
+                start_copy(side, item, 1)
+    @pl.when(gives)
+    def _():
+        give.start()
+
     load_v.wait()
     for copy in v_copies + d_copies:
         copy.start()
@@ -204,18 +260,26 @@
     def _():
         greet(down, gx=gx - 2)
 
-    for side in range(2):
-        start_u(side, range(quarter), True)
     @pl.when(ends)
     def _():
+        for other in range(2):
+            for side in range(2):
+                start_u(side, other, True)
         for side in range(2):
-            start_u(side, range(1, quarter), False)
+            start_u(side, 1, False)
+
+    @pl.when(takes)
+    def _():
+        arrived(u_guest.at[pl.ds(0, 2)], send_sem.at[3], recv_sem.at[2]).wait_recv()
+        guest_on.start()
+        u_copy(*SHARED, pl.ds(0, width_y)).start()
 
     greet(pair_sem.at[0], gy=near)
     pl.semaphore_wait(pair_sem.at[0], 1)
     for hop in range(1, n_gy // 2):
         greet(pair_sem.at[hop], gy=far_from)
         pl.semaphore_wait(pair_sem.at[hop], 1)
+
 
     pltpu.make_async_copy(sep_s, sep_s, sep_sem.at[0]).wait()
     lane = lax.broadcasted_iota(jnp.int32, (1, LANES), 1)
@@ -252,17 +316,7 @@
 
     pltpu.make_async_copy(v_hbm, v_own, load_sem.at[2]).wait()
 
-    def arrived(ref, send, recv):
-        return pltpu.make_async_remote_copy(
-            src_ref=ref,
-            dst_ref=ref,
-            send_sem=send,
-            recv_sem=recv,
-            device_id={"gx": chip_first + 1 - core},
-            device_id_type=MESH,
-        )
-
-    all_u = arrived(u_own, send_sem.at[0], recv_sem.at[0])
+    all_u = arrived(v_own.at[pl.ds(0, planes - 1)], send_sem.at[0], recv_sem.at[0])
     all_v = arrived(v_own, send_sem.at[1], recv_sem.at[1])
     all_d = arrived(u_wide.at[0, :, pl.ds(0, 2)], send_sem.at[2], recv_sem.at[0])
     all_v.wait_recv()
@@ -273,19 +327,61 @@
     gram_0 = product(left, left, ((0,), (0,)))
     gram_1 = product(left, (high[cells:], low[cells:]), ((0,), (0,)))
     gram_y = jnp.concatenate([gram_0, gram_1], axis=1)
-    rest = lag_sums(gram_y, lags_y, width_y) + row_z
+    sums_y = jnp.where(lags_y < 0, 0.0, lag_sums(folded(gram_y, width_y + LANES), lags_y))
+    row_z = row_z + jnp.sum(sums_y, axis=0, keepdims=True)
 
     all_d.wait_recv()
-    gram_x = None
+    pair_x = 2 * width_x
+    column = lax.broadcasted_iota(jnp.int32, (1, width_y), 1)
+    keep = (column < width_y // 2) | ~short
+
+    def block(side, item, slot):
+        cells = u_wide[side, item, slot : slot + 2].reshape(pair_x, width_y)
+        return split(jnp.where(keep, cells, 0.0) if (side, item) == SHARED[:2] else cells)
+
+    by_rows = ((1,), (1,))
+    def add(total, term):
+        return term if total is None else total + term
+
+    gram = None
+    for side in range(2):
+        for item in range(quarter):
+            own = block(side, item, 2 * side)
+            gram = add(gram, product(own, own, by_rows))
+    sums_x = lag_sums(gram, lags_x)
+
+    gram = None
     for item in range(quarter):
         for side in range(2):
-            theirs = u_wide.at[side, item, pl.ds(2 - 2 * side, 2)]
-            arrived(theirs, send_sem.at[0], u_recv.at[side, item]).wait_recv()
-            pair = split(u_wide[side, item].reshape(4 * width_x, width_y))
-            lower = (pair[0][: 2 * width_x], pair[1][: 2 * width_x])
-            term = product(lower, pair, ((1,), (1,)))
-            gram_x = term if gram_x is None else gram_x + term
-    mine = lag_sums(gram_x, lags_x, 2 * width_x) + rest
+            own = block(side, item, 2 * side)
+            recv = u_recv.at[side, item]
+            whole = arrived(u_wide.at[side, item, pl.ds(2 - 2 * side, 2)], send_sem.at[0], recv)
+            if (side, item) == SHARED[:2]:
+                @pl.when(short)
+                def _():
+                    arrived(u_guest.at[pl.ds(0, 2)], send_sem.at[0], recv).wait_recv()
+
+                @pl.when(~short)
+                def _():
+                    whole.wait_recv()
+            else:
+                whole.wait_recv()
+            theirs = block(side, item, 2 - 2 * side)
+            lower, upper = (own, theirs) if side == 0 else (theirs, own)
+            gram = add(gram, product(lower, upper, by_rows))
+    sums_x = sums_x + lag_sums(gram, lags_x - pair_x)
+
+    @pl.when(takes)
+    def _():
+        guest_on.wait_recv()
+        lower = split(u_guest[2:].reshape(pair_x, width_y // 2))
+        upper = split(u_guest[:2].reshape(pair_x, width_y // 2))
+        guest_sums[...] = lag_sums(product(upper, upper, by_rows), lags_x) + lag_sums(
+            product(lower, upper, by_rows), lags_x - pair_x
+        )
+
+    sums_x = sums_x + guest_sums[...]
+    mine = jnp.sum(jnp.where(lags_x < 0, 0.0, sums_x), axis=0, keepdims=True) + row_z
 
     count = n_gx * n_gy
     me = gx * n_gy + gy
@@ -312,6 +408,13 @@
     all_rows = arrived(rows.at[pl.ds(0, count - 1)], row_sem.at[0], row_sem.at[1])
     for copy in (all_u, all_v, all_d):
         copy.wait_send()
+
+    arrived(u_guest.at[pl.ds(0, 2)], send_sem.at[3], recv_sem.at[2]).wait_send()
+
+    @pl.when(takes)
+    def _():
+        guest_on.wait_send()
+
     all_rows.wait_recv()
     total = jnp.sum(rows[...], axis=0)
 
@@ -342,15 +445,17 @@
             pltpu.VMEM(block, jnp.float32),
             pltpu.VMEM(block, jnp.float32),
             pltpu.VMEM((2, quarter, 4, width_x, width_y), jnp.float32),
+            pltpu.VMEM((4, width_x, width_y // 2), jnp.float32),
+            pltpu.VMEM((8, LANES), jnp.float32),
             pltpu.VMEM((3, half, width_x, width_y), jnp.float32),
             pltpu.SMEM((3, seps), jnp.int32),
             pltpu.VMEM((n_gx * n_gy, 1, LANES), jnp.float32),
             dma((quarter,)),
             dma((3,)),
             dma((1,)),
-            dma((3,)),
+            dma((5,)),
             dma((2, quarter)),
-            dma((2,)),
+            dma((4,)),
             dma((2,)),
             pltpu.SemaphoreType.REGULAR((2,)),
             pltpu.SemaphoreType.REGULAR((n_gy // 2,)),

time: 23.5 us -> 22.9 us (0.974)
  Pallas kernels: 22.7 us -> 22.2 us
    pallas_call x1, Pallas kernels: 22.7 us -> 22.2 us  [local(): pl.pallas_call(functools.partial(kernel, n_gx, n_gy), out_shape=pltpu.VME...]
where the time goes in v2:
time: 22.9 us; the launch traced here: 22.8 us
  Pallas kernels  22.2 us (97%)
  local copies, waits for them, and re-layouts  0.58 us (3%)
    pallas_call x1, Pallas kernels, local(): pl.pallas_call(functools.partial(kernel, n_gx, n_gy), out_shape=pltpu.VME...  22.2 us
    unnamed x1, local copies, waits for them, and re-layouts  0.58 us

profile of v2, /device:TPU:0, one launch (start us, length us, event | category | flops | bytes accessed | tf_op | source)
XLA Modules:
  0.0 22.8 jit_solution(1194592528054604024)
XLA Ops:
  0.0 22.2 %shard_map.64 = f32[3,16]{1,0:T(4,128)S(1)} custom-call(f32[2,2,2,64,256]{4,3,2,1,0:T(8,128)} %bitcast.1, f32[8,64,256]{2,1,0:T(8,128)} %v_hbm.1, f32[8,64,256]{2,1,0:T(8,128)} %w_hbm.1, s32[16]{0:T(128)} %sep_x_hbm.1, s32[16]{0:T(128)} %sep_y_hbm.1, s32[16]{0:T(128)} %sep_z_hbm.1), custom_call_target="tpu_custom_call" | custom-call | tf_op jit(solution)/shard_map/pallas_call | solution.py:438
  22.2 0.6 %copy.8 = f32[3,16]{1,0:T(4,128)} copy(f32[3,16]{1,0:T(4,128)S(1)} %shard_map.64) | data formatting | bytes 384
